TPU v7x, 32 devices: a whole 2x2x4 slice. The times are simulated.
32 devices in a mesh: dp: 4 (over z), feat: 8 (over y, x, core).
Axes of the slice: x: 2, y: 2, z: 4, core: 2. Of those that a mesh axis runs over, the one named last changes fastest.
Arguments:
- features: float32 [4096, 8192], P('dp', 'feat'), may hold values from -0.0625 to 0.0625
- labels: int32 [4096], P('dp'), may hold values from -1 to 1, as said below
- weights: float32 [8192], P('feat'), may hold values from -6 to 6
Outputs:
- gradient: float32 [8192], P('feat')
- newton_step: float32 [8192], P('feat')
- residual: float32 [8192], P('feat')
Inputs may be any that keep to these rules, and one draw needn't show every extreme that they name: `labels`: every label is -1 or +1.
All inputs are finite; a program needn't handle non-finite values.
Results may differ from a plain program's by a relative error of at most 0.0003.
Values sent between devices are 32-bit elements; how exact they have to be, the bound alone decides.
A program may use at most 64 MiB of HBM per device.

v0:
```python
import jax
import jax.numpy as jnp
from jax import lax
from jax.sharding import PartitionSpec as P

CG_STEPS = 3
PENALTY = 4.0
HIGH = lax.Precision.HIGHEST


def squares(residual):
    return lax.psum(jnp.sum(residual * residual), "feat")


def local(features, labels, weights):
    y = labels.astype(jnp.float32)
    margin = y * lax.psum(jnp.dot(features, weights, precision=HIGH), "feat")
    sig = 1.0 / (1.0 + jnp.exp(-margin))
    local_grad = jnp.dot((sig - 1.0) * y, features, precision=HIGH)
    gradient = weights + PENALTY * lax.psum(local_grad, "dp")
    curv = PENALTY * sig * (1.0 - sig)
    newton_step = jnp.zeros_like(weights)
    residual = -gradient
    direction = residual
    rr = squares(residual)
    for step in range(CG_STEPS):
        image_rows, dir_sq = lax.psum(
            (jnp.dot(features, direction, precision=HIGH), jnp.sum(direction * direction)), "feat"
        )
        weighted = curv * image_rows
        back, quad = lax.psum(
            (jnp.dot(weighted, features, precision=HIGH), jnp.sum(weighted * image_rows)), "dp"
        )
        curvature = dir_sq + quad
        image = direction + back
        alpha = rr / curvature
        newton_step = newton_step + alpha * direction
        residual = residual - alpha * image
        fresh = squares(residual)
        direction = residual + fresh / rr * direction
        rr = fresh
    return (gradient, newton_step, residual)


def solution(mesh):
    placed = (P("dp", "feat"), P("dp"), P("feat"))
    return jax.shard_map(
        local,
        mesh=mesh,
        in_specs=placed,
        out_specs=(P("feat"), P("feat"), P("feat")),
        check_vma=False,
    )
```

profile of v0, /device:TPU:0, one launch (start us, length us, event | category | flops | bytes accessed | tf_op | source)
XLA Modules:
  0.0 174.1 jit_solution(13997829717275814949)
XLA Ops:
  0.6 0.0 copy-start.2
  0.6 0.0 copy-start.1
  0.7 5.8 %fusion.3 = f32[1,1024]{1,0:T(1,128)S(1)} fusion(f32[1024,1024]{1,0:T(8,128)} %param.3, f32[1024,1]{0,1:T(1,128)} %bitcast.34), kind=kOutput, calls=%fused_computation.21 | convolution fusion | flops 12582912 | bytes 4202496 | tf_op jit(solution)/shard_map/dot_general | solution.py:17
  6.4 15.2 %psum.115 = f32[1024]{0:T(1024)S(1)} all-reduce(f32[1024]{0:T(1024)S(1)} %bitcast.45), channel_id=1, replica_groups=mesh['dp'=4,'feat'=8] {'feat'}, use_global_device_ids=true, to_apply=%region_0.0 | all-reduce | flops 1024 | bytes 8192 | tf_op jit(solution)/shard_map/psum | solution.py:17
  21.6 0.0 copy-done.2
  21.6 4.3 %fusion.4 = f32[1,1024]{1,0:T(1,128)S(1)} fusion(f32[1024,1]{0,1:T(1,128)S(1)} %bitcast.47, f32[1024,1024]{1,0:T(8,128)} %param.3), kind=kOutput, calls=%fused_computation.22 | convolution fusion | flops 12582912 | bytes 4202496 | tf_op jit(solution)/shard_map/dot_general | solution.py:19
  25.9 11.9 %psum.116 = f32[1024]{0:T(1024)S(1)} all-reduce(f32[1024]{0:T(1024)S(1)} %bitcast.44), channel_id=1, replica_groups=mesh['dp'=4,'feat'=8] {'dp'}, use_global_device_ids=true, to_apply=%region_1.0 | all-reduce | flops 1024 | bytes 8192 | tf_op jit(solution)/shard_map/psum | solution.py:20
  37.8 0.0 copy-done.1
  37.8 0.6 multiply_reduce_fusion.7
  38.4 5.6 %fusion.5 = f32[1,1024]{1,0:T(1,128)S(1)} fusion(f32[1024,1]{0,1:T(1,128)S(1)} %bitcast.46, f32[1024,1024]{1,0:T(8,128)} %param.3), kind=kOutput, calls=%fused_computation.23 | convolution fusion | flops 12582912 | bytes 4202496 | tf_op jit(solution)/shard_map/dot_general | solution.py:28
  44.1 12.8 %all-reduce.2 = (f32[1024]{0:T(1024)S(1)}, f32[]{:T(128)}) all-reduce(f32[1024]{0:T(1024)S(1)} %bitcast.38, f32[]{:T(128)} %get-tuple-element.21), channel_id=1, replica_groups=mesh['dp'=4,'feat'=8] {'feat'}, use_global_device_ids=true, to_apply=%region_4.0 | all-reduce | flops 1025 | bytes 8200 | tf_op jit(solution)/shard_map/psum | solution.py:27
  56.8 0.6 multiply_reduce_fusion.6
  57.4 4.3 %fusion.6 = f32[1,1024]{1,0:T(1,128)S(1)} fusion(f32[1024,1]{0,1:T(1,128)S(1)} %bitcast.36, f32[1024,1024]{1,0:T(8,128)} %param.3), kind=kOutput, calls=%fused_computation.24 | convolution fusion | flops 12582912 | bytes 4202496 | tf_op jit(solution)/shard_map/dot_general | solution.py:32
  61.7 9.1 %all-reduce.5 = (f32[1024]{0:T(1024)S(1)}, f32[]{:T(128)}) all-reduce(f32[1024]{0:T(1024)S(1)} %bitcast.39, f32[]{:T(128)} %get-tuple-element.29), channel_id=1, replica_groups=mesh['dp'=4,'feat'=8] {'dp'}, use_global_device_ids=true, to_apply=%region_7.0 | all-reduce | flops 1025 | bytes 8200 | tf_op jit(solution)/shard_map/psum | solution.py:31
  72.7 0.6 multiply_reduce_fusion.5
  73.3 12.6 %psum.121 = f32[]{:T(128)} all-reduce(f32[]{:T(128)} %multiply_reduce_fusion.5), channel_id=1, replica_groups=mesh['dp'=4,'feat'=8] {'feat'}, use_global_device_ids=true, to_apply=%region_9.0 | all-reduce | flops 1 | bytes 8 | tf_op jit(solution)/shard_map/psum | solution.py:12
  87.3 0.6 multiply_reduce_fusion.4
  87.9 5.6 %fusion.7 = f32[1,1024]{1,0:T(1,128)S(1)} fusion(f32[1024,1]{0,1:T(1,128)S(1)} %bitcast.32, f32[1024,1024]{1,0:T(8,128)} %param.3), kind=kOutput, calls=%fused_computation.25 | convolution fusion | flops 12582912 | bytes 4202496 | tf_op jit(solution)/shard_map/dot_general | solution.py:28
  93.5 12.8 %all-reduce.1 = (f32[1024]{0:T(1024)S(1)}, f32[]{:T(128)}) all-reduce(f32[1024]{0:T(1024)S(1)} %bitcast.42, f32[]{:T(128)} %get-tuple-element.19), channel_id=1, replica_groups=mesh['dp'=4,'feat'=8] {'feat'}, use_global_device_ids=true, to_apply=%region_12.0 | all-reduce | flops 1025 | bytes 8200 | tf_op jit(solution)/shard_map/psum | solution.py:27
  106.3 0.7 multiply_reduce_fusion.3
  107.0 4.3 %fusion.8 = f32[1,1024]{1,0:T(1,128)S(1)} fusion(f32[1024,1]{0,1:T(1,128)S(1)} %bitcast.37, f32[1024,1024]{1,0:T(8,128)} %param.3), kind=kOutput, calls=%fused_computation.26 | convolution fusion | flops 12582912 | bytes 4202496 | tf_op jit(solution)/shard_map/dot_general | solution.py:32
  111.2 11.1 %all-reduce.4 = (f32[1024]{0:T(1024)S(1)}, f32[]{:T(128)}) all-reduce(f32[1024]{0:T(1024)S(1)} %bitcast.40, f32[]{:T(128)} %get-tuple-element.27), channel_id=1, replica_groups=mesh['dp'=4,'feat'=8] {'dp'}, use_global_device_ids=true, to_apply=%region_15.0 | all-reduce | flops 1025 | bytes 8200 | tf_op jit(solution)/shard_map/psum | solution.py:31
  124.2 0.6 multiply_reduce_fusion.2
  124.8 12.4 %psum.126 = f32[]{:T(128)} all-reduce(f32[]{:T(128)} %get-tuple-element.17), channel_id=1, replica_groups=mesh['dp'=4,'feat'=8] {'feat'}, use_global_device_ids=true, to_apply=%region_17.0 | all-reduce | flops 1 | bytes 8 | tf_op jit(solution)/shard_map/psum | solution.py:12
  138.6 0.6 multiply_reduce_fusion.1
  139.2 5.6 %fusion.9 = f32[1,1024]{1,0:T(1,128)S(1)} fusion(f32[1024,1]{0,1:T(1,128)S(1)} %bitcast.33, f32[1024,1024]{1,0:T(8,128)} %param.3), kind=kOutput, calls=%fused_computation.27 | convolution fusion | flops 12582912 | bytes 4202496 | tf_op jit(solution)/shard_map/dot_general | solution.py:28
  144.8 12.7 %all-reduce = (f32[]{:T(128)}, f32[1024]{0:T(1024)S(1)}) all-reduce(f32[]{:T(128)} %get-tuple-element.15, f32[1024]{0:T(1024)S(1)} %bitcast.43), channel_id=1, replica_groups=mesh['dp'=4,'feat'=8] {'feat'}, use_global_device_ids=true, to_apply=%region_19.0 | all-reduce | flops 1025 | bytes 8200 | tf_op jit(solution)/shard_map/psum | solution.py:27
  157.6 0.7 fusion
  158.3 4.3 %fusion.10 = f32[1,1024]{1,0:T(1,128)S(1)} fusion(f32[1024,1]{0,1:T(1,128)S(1)} %bitcast.35, f32[1024,1024]{1,0:T(8,128)} %param.3), kind=kOutput, calls=%fused_computation.28 | convolution fusion | flops 12582912 | bytes 4202496 | tf_op jit(solution)/shard_map/dot_general | solution.py:32
  162.5 9.1 %all-reduce.3 = (f32[]{:T(128)}, f32[1024]{0:T(1024)S(1)}) all-reduce(f32[]{:T(128)} %get-tuple-element.26, f32[1024]{0:T(1024)S(1)} %bitcast.41), channel_id=1, replica_groups=mesh['dp'=4,'feat'=8] {'dp'}, use_global_device_ids=true, to_apply=%region_22.0 | all-reduce | flops 1025 | bytes 8200 | tf_op jit(solution)/shard_map/psum | solution.py:31
  173.5 0.0 copy-done
  173.5 0.6 multiply_subtract_fusion
  (3 shorter events, 0.0 us)
Async XLA Ops:
  0.6 20.9 %copy-start.2 = (s32[1024]{0:T(1024)S(1)}, s32[1024]{0:T(1024)}, u32[]{:S(2)}) copy-start(s32[1024]{0:T(1024)} %param.4) | copy-start | bytes 12292
  0.6 37.2 %copy-start.1 = (f32[1024]{0:T(1024)S(1)}, f32[1024]{0:T(1024)}, u32[]{:S(2)}) copy-start(f32[1024]{0:T(1024)} %param.5) | copy-start | bytes 12292
  38.4 135.1 %copy-start = (f32[1024]{0:T(1024)}, f32[1024]{0:T(1024)S(1)}, u32[]{:S(2)}) copy-start(f32[1024]{0:T(1024)S(1)} %get-tuple-element.22) | copy-start | bytes 12292
where the time goes:
time: 175 us; the launch traced here: 174 us
  blocking collectives  120 us (69%)
  matrix products  39.8 us (23%)
  between operations  9.03 us (5%)
  other arithmetic  5.6 us (3%)
    psum x3, blocking collectives, local(): lax.psum((jnp.dot(features, direction, precision=HIGH), jnp.sum(direction...  38.2 us
    psum x3, blocking collectives, local(): lax.psum((jnp.dot(weighted, features, precision=HIGH), jnp.sum(weighted *...  29.4 us
    psum x2, blocking collectives, squares(): return lax.psum(jnp.sum(residual * residual), 'feat')  25 us
    dot_general x3, matrix products, local(): jnp.dot(features, direction, precision=HIGH)  16.9 us
    psum x1, blocking collectives, local(): margin = y * lax.psum(jnp.dot(features, weights, precision=HIGH), 'feat')  15.2 us
    dot_general x3, matrix products, local(): jnp.dot(weighted, features, precision=HIGH)  12.8 us
    psum x1, blocking collectives, local(): gradient = weights + PENALTY * lax.psum(local_grad, 'dp')  11.9 us
    dot_general x1, matrix products, local(): margin = y * lax.psum(jnp.dot(features, weights, precision=HIGH), 'feat')  5.76 us

commit v1 on v0

--- a/solution.py
+++ b/solution.py
@@ -8,13 +8,19 @@
 HIGH = lax.Precision.HIGHEST
 
 
+def gather_and_add(block, axis):
+    parts = lax.all_gather(block, axis, axis=0, tiled=False)
+    result = parts.sum(axis=0)
+    return result
+
+
 def squares(residual):
     return lax.psum(jnp.sum(residual * residual), "feat")
 
 
 def local(features, labels, weights):
     y = labels.astype(jnp.float32)
-    margin = y * lax.psum(jnp.dot(features, weights, precision=HIGH), "feat")
+    margin = y * gather_and_add(jnp.dot(features, weights, precision=HIGH), "feat")
     sig = 1.0 / (1.0 + jnp.exp(-margin))
     local_grad = jnp.dot((sig - 1.0) * y, features, precision=HIGH)
     gradient = weights + PENALTY * lax.psum(local_grad, "dp")

time: 175 us -> 170 us (0.971)
  blocking collectives: 120 us -> 115 us
    psum x1 -> x0, blocking collectives: 15.2 us -> none  [local(): margin = y * lax.psum(jnp.dot(features, weights, precision=HIGH), 'feat')]
    all_gather x0 -> x1, blocking collectives: none -> 10.6 us  [gather_and_add(): parts = lax.all_gather(block, axis, axis=0, tiled=False)]
where the time goes in v1:
time: 170 us; the launch traced here: 169 us
  blocking collectives  115 us (68%)
  matrix products  39.8 us (23%)
  between operations  9.04 us (5%)
  other arithmetic  5.62 us (3%)
    psum x3, blocking collectives, local(): lax.psum((jnp.dot(features, direction, precision=HIGH), jnp.sum(direction...  38.1 us
    psum x3, blocking collectives, local(): lax.psum((jnp.dot(weighted, features, precision=HIGH), jnp.sum(weighted *...  29.4 us
    psum x2, blocking collectives, squares(): return lax.psum(jnp.sum(residual * residual), 'feat')  25 us
    dot_general x3, matrix products, local(): jnp.dot(features, direction, precision=HIGH)  16.9 us
    dot_general x3, matrix products, local(): jnp.dot(weighted, features, precision=HIGH)  12.8 us
    psum x1, blocking collectives, local(): gradient = weights + PENALTY * lax.psum(local_grad, 'dp')  11.9 us
    all_gather x1, blocking collectives, gather_and_add(): parts = lax.all_gather(block, axis, axis=0, tiled=False)  10.6 us
    dot_general x1, matrix products, local(): jnp.dot(features, weights, precision=HIGH)  5.76 us

profile of v1, /device:TPU:0, one launch (start us, length us, event | category | flops | bytes accessed | tf_op | source)
XLA Modules:
  0.0 169.4 jit_solution(1365845633718539054)
XLA Ops:
  0.6 0.0 copy-start.2
  0.6 0.0 copy-start.1
  0.7 5.8 %fusion.3 = f32[1,1024]{1,0:T(1,128)S(1)} fusion(f32[1024,1024]{1,0:T(8,128)} %param.3, f32[1024,1]{0,1:T(1,128)} %bitcast.34), kind=kOutput, calls=%fused_computation.21 | convolution fusion | flops 12582912 | bytes 4202496 | tf_op jit(solution)/shard_map/dot_general | solution.py:23
  6.4 10.6 %all-gather = f32[8192]{0:T(1024)S(1)} all-gather(f32[1024]{0:T(1024)S(1)} %bitcast.38), channel_id=2, replica_groups=mesh['dp'=4,'feat'=8] {'feat'}, dimensions={0}, use_global_device_ids=true | all-gather | bytes 36864 | tf_op jit(solution)/shard_map/all_gather | solution.py:12
  17.0 0.0 copy-done.2
  17.1 4.3 %fusion.4 = f32[1,1024]{1,0:T(1,128)S(1)} fusion(f32[1024,1]{0,1:T(1,128)S(1)} %bitcast.47, f32[1024,1024]{1,0:T(8,128)} %param.3), kind=kOutput, calls=%fused_computation.22 | convolution fusion | flops 12582912 | bytes 4202496 | tf_op jit(solution)/shard_map/dot_general | solution.py:25
  21.3 11.9 %psum.108 = f32[1024]{0:T(1024)S(1)} all-reduce(f32[1024]{0:T(1024)S(1)} %bitcast.45), channel_id=1, replica_groups=mesh['dp'=4,'feat'=8] {'dp'}, use_global_device_ids=true, to_apply=%region_1.0 | all-reduce | flops 1024 | bytes 8192 | tf_op jit(solution)/shard_map/psum | solution.py:26
  33.3 0.0 copy-done.1
  33.3 0.6 multiply_reduce_fusion.7
  33.9 5.6 %fusion.5 = f32[1,1024]{1,0:T(1,128)S(1)} fusion(f32[1024,1]{0,1:T(1,128)S(1)} %bitcast.46, f32[1024,1024]{1,0:T(8,128)} %param.3), kind=kOutput, calls=%fused_computation.23 | convolution fusion | flops 12582912 | bytes 4202496 | tf_op jit(solution)/shard_map/dot_general | solution.py:34
  39.5 12.7 %all-reduce.2 = (f32[1024]{0:T(1024)S(1)}, f32[]{:T(128)}) all-reduce(f32[1024]{0:T(1024)S(1)} %bitcast.39, f32[]{:T(128)} %get-tuple-element.21), channel_id=1, replica_groups=mesh['dp'=4,'feat'=8] {'feat'}, use_global_device_ids=true, to_apply=%region_4.0 | all-reduce | flops 1025 | bytes 8200 | tf_op jit(solution)/shard_map/psum | solution.py:33
  52.3 0.6 multiply_reduce_fusion.6
  52.9 4.3 %fusion.6 = f32[1,1024]{1,0:T(1,128)S(1)} fusion(f32[1024,1]{0,1:T(1,128)S(1)} %bitcast.36, f32[1024,1024]{1,0:T(8,128)} %param.3), kind=kOutput, calls=%fused_computation.24 | convolution fusion | flops 12582912 | bytes 4202496 | tf_op jit(solution)/shard_map/dot_general | solution.py:38
  57.2 9.1 %all-reduce.5 = (f32[1024]{0:T(1024)S(1)}, f32[]{:T(128)}) all-reduce(f32[1024]{0:T(1024)S(1)} %bitcast.40, f32[]{:T(128)} %get-tuple-element.29), channel_id=1, replica_groups=mesh['dp'=4,'feat'=8] {'dp'}, use_global_device_ids=true, to_apply=%region_7.0 | all-reduce | flops 1025 | bytes 8200 | tf_op jit(solution)/shard_map/psum | solution.py:37
  68.2 0.6 multiply_reduce_fusion.5
  68.8 12.6 %psum.113 = f32[]{:T(128)} all-reduce(f32[]{:T(128)} %multiply_reduce_fusion.5), channel_id=1, replica_groups=mesh['dp'=4,'feat'=8] {'feat'}, use_global_device_ids=true, to_apply=%region_9.0 | all-reduce | flops 1 | bytes 8 | tf_op jit(solution)/shard_map/psum | solution.py:18
  82.8 0.6 multiply_reduce_fusion.4
  83.4 5.6 %fusion.7 = f32[1,1024]{1,0:T(1,128)S(1)} fusion(f32[1024,1]{0,1:T(1,128)S(1)} %bitcast.32, f32[1024,1024]{1,0:T(8,128)} %param.3), kind=kOutput, calls=%fused_computation.25 | convolution fusion | flops 12582912 | bytes 4202496 | tf_op jit(solution)/shard_map/dot_general | solution.py:34
  89.0 12.7 %all-reduce.1 = (f32[1024]{0:T(1024)S(1)}, f32[]{:T(128)}) all-reduce(f32[1024]{0:T(1024)S(1)} %bitcast.43, f32[]{:T(128)} %get-tuple-element.19), channel_id=1, replica_groups=mesh['dp'=4,'feat'=8] {'feat'}, use_global_device_ids=true, to_apply=%region_12.0 | all-reduce | flops 1025 | bytes 8200 | tf_op jit(solution)/shard_map/psum | solution.py:33
  101.7 0.7 multiply_reduce_fusion.3
  102.4 4.3 %fusion.8 = f32[1,1024]{1,0:T(1,128)S(1)} fusion(f32[1024,1]{0,1:T(1,128)S(1)} %bitcast.37, f32[1024,1024]{1,0:T(8,128)} %param.3), kind=kOutput, calls=%fused_computation.26 | convolution fusion | flops 12582912 | bytes 4202496 | tf_op jit(solution)/shard_map/dot_general | solution.py:38
  106.6 11.1 %all-reduce.4 = (f32[1024]{0:T(1024)S(1)}, f32[]{:T(128)}) all-reduce(f32[1024]{0:T(1024)S(1)} %bitcast.41, f32[]{:T(128)} %get-tuple-element.27), channel_id=1, replica_groups=mesh['dp'=4,'feat'=8] {'dp'}, use_global_device_ids=true, to_apply=%region_15.0 | all-reduce | flops 1025 | bytes 8200 | tf_op jit(solution)/shard_map/psum | solution.py:37
  119.6 0.6 multiply_reduce_fusion.2
  120.2 12.4 %psum.118 = f32[]{:T(128)} all-reduce(f32[]{:T(128)} %get-tuple-element.17), channel_id=1, replica_groups=mesh['dp'=4,'feat'=8] {'feat'}, use_global_device_ids=true, to_apply=%region_17.0 | all-reduce | flops 1 | bytes 8 | tf_op jit(solution)/shard_map/psum | solution.py:18
  134.0 0.6 multiply_reduce_fusion.1
  134.6 5.6 %fusion.9 = f32[1,1024]{1,0:T(1,128)S(1)} fusion(f32[1024,1]{0,1:T(1,128)S(1)} %bitcast.33, f32[1024,1024]{1,0:T(8,128)} %param.3), kind=kOutput, calls=%fused_computation.27 | convolution fusion | flops 12582912 | bytes 4202496 | tf_op jit(solution)/shard_map/dot_general | solution.py:34
  140.2 12.7 %all-reduce = (f32[]{:T(128)}, f32[1024]{0:T(1024)S(1)}) all-reduce(f32[]{:T(128)} %get-tuple-element.15, f32[1024]{0:T(1024)S(1)} %bitcast.44), channel_id=1, replica_groups=mesh['dp'=4,'feat'=8] {'feat'}, use_global_device_ids=true, to_apply=%region_19.0 | all-reduce | flops 1025 | bytes 8200 | tf_op jit(solution)/shard_map/psum | solution.py:33
  152.9 0.7 fusion
  153.6 4.3 %fusion.10 = f32[1,1024]{1,0:T(1,128)S(1)} fusion(f32[1024,1]{0,1:T(1,128)S(1)} %bitcast.35, f32[1024,1024]{1,0:T(8,128)} %param.3), kind=kOutput, calls=%fused_computation.28 | convolution fusion | flops 12582912 | bytes 4202496 | tf_op jit(solution)/shard_map/dot_general | solution.py:38
  157.9 9.1 %all-reduce.3 = (f32[]{:T(128)}, f32[1024]{0:T(1024)S(1)}) all-reduce(f32[]{:T(128)} %get-tuple-element.26, f32[1024]{0:T(1024)S(1)} %bitcast.42), channel_id=1, replica_groups=mesh['dp'=4,'feat'=8] {'dp'}, use_global_device_ids=true, to_apply=%region_22.0 | all-reduce | flops 1025 | bytes 8200 | tf_op jit(solution)/shard_map/psum | solution.py:37
  168.8 0.0 copy-done
  168.8 0.6 multiply_subtract_fusion
  (5 shorter events, 0.0 us)
Async XLA Ops:
  0.6 16.4 %copy-start.2 = (s32[1024]{0:T(1024)S(1)}, s32[1024]{0:T(1024)}, u32[]{:S(2)}) copy-start(s32[1024]{0:T(1024)} %param.4) | copy-start | bytes 12292
  0.6 32.6 %copy-start.1 = (f32[1024]{0:T(1024)S(1)}, f32[1024]{0:T(1024)}, u32[]{:S(2)}) copy-start(f32[1024]{0:T(1024)} %param.5) | copy-start | bytes 12292
  33.9 134.9 %copy-start = (f32[1024]{0:T(1024)}, f32[1024]{0:T(1024)S(1)}, u32[]{:S(2)}) copy-start(f32[1024]{0:T(1024)S(1)} %get-tuple-element.22) | copy-start | bytes 12292
